TPU v7x, 32 devices: a whole 2x2x4 slice. The times are simulated.
32 devices in a mesh: row: 8 (over y, x, core), col: 4 (over z).
Axes of the slice: x: 2, y: 2, z: 4, core: 2. Of those that a mesh axis runs over, the one named last changes fastest.
Arguments:
- temps: bfloat16 [12, 64, 16384], P(None, None, ('row', 'col')), may hold values from -6 to 6
- sensors: int32 [12, 512], replicated, may hold values from 0 to 16383
Outputs:
- corr: bfloat16 [512, 16384], P('col', 'row')
Inputs may be any that keep to these rules, and one draw needn't show every extreme that they name: `sensors`: each entry is a pixel index of its tier; candidates may repeat.
All inputs are finite; a program needn't handle non-finite values.
Results may differ from a plain program's by a relative error of at most 0.001.
Values may be sent and summed in bfloat16 or wider, within the bound.
A program may use at most 64 MiB of HBM per device.

v0:
```python
import jax
import jax.numpy as jnp
from jax import lax
from jax.sharding import PartitionSpec as P


def select_columns(fields, sensor_rows, first_pixel):
    width = fields.shape[2]
    offsets = sensor_rows - first_pixel
    pixel_ids = lax.broadcasted_iota(jnp.int32, (width, sensor_rows.shape[1]), 0)

    def one_tier(pair):
        tier_fields, tier_offsets = pair
        selector = (pixel_ids == tier_offsets[None, :]).astype(jnp.bfloat16)
        return jnp.dot(tier_fields, selector, preferred_element_type=jnp.float32)

    return lax.map(one_tier, (fields, offsets))


def body(temps, sensors):
    col_count = lax.axis_size("col")
    first_pixel = (lax.axis_index("row") * col_count + lax.axis_index("col")) * temps.shape[2]
    local_values = select_columns(temps, sensors, first_pixel)
    owned = lax.psum_scatter(
        local_values.astype(jnp.bfloat16), "col", scatter_dimension=2, tiled=True
    )
    readings = lax.psum(owned, "row").astype(jnp.float32).astype(jnp.bfloat16)
    scale_factor = 1.0 / jnp.sqrt(jnp.float32(temps.shape[0] * temps.shape[1]))
    summed = jnp.einsum(
        "tsc,tsp->cp",
        lax.all_gather(readings, "col", axis=2, tiled=True),
        temps,
        preferred_element_type=jnp.float32,
    )
    rounded = (summed * scale_factor).astype(jnp.bfloat16)
    return lax.all_to_all(rounded, "col", split_axis=0, concat_axis=1, tiled=True)


def solution(mesh):
    placed = (P(None, None, ("row", "col")), P())
    return jax.shard_map(
        body, mesh=mesh, in_specs=placed, out_specs=P("col", "row"), check_vma=False
    )
```

profile of v0, /device:TPU:0, one launch (start us, length us, event | category | flops | bytes accessed | tf_op | source)
XLA Modules:
  0.0 149.4 jit_solution(5405462871860880620)
XLA Ops:
  6.5 0.0 reduce-scatter.4.cloned.1.call-start
  6.5 0.8 broadcast_subtract_fusion
  7.3 14.2 %while.11 = (s32[]{:T(128)}, bf16[12,64,512]{2,1,0:T(8,128)(2,1)S(1)}, bf16[12,64,512]{2,1,0:T(8,128)(2,1)}, s32[12,512]{1,0:T(8,128)S(1)}, s32[]{:T(128)}) while((s32[]{:T(128)}, bf16[12,64,512]{2,1,0:T(8,128)(2,1)S(1)}, bf16[12,64,512]{2,1,0:T(8,128)(2,1)}, s32[12,512]{1,0:T(8,128)S(1)}, s32[]{:T(128)}) %tuple.21), condition=%wide.region_1.2_spmd.clone, body=%wide.region_0.1_spmd.clone.sunk | while | flops 33816576 | bytes 203849 | solution.py:17
  7.3 1.2 fusion.14
  8.5 1.2 fusion.14
  9.7 1.2 fusion.14
  10.9 1.2 fusion.14
  12.1 1.2 fusion.14
  13.2 1.2 fusion.14
  14.4 1.2 fusion.14
  15.6 1.2 fusion.14
  16.8 1.2 fusion.14
  18.0 1.2 fusion.14
  19.2 1.2 fusion.14
  20.4 1.2 fusion.14
  21.5 2.0 %copy.5 = bf16[12,64,512]{1,0,2:T(8,128)(2,1)S(1)} copy(bf16[12,64,512]{2,1,0:T(8,128)(2,1)S(1)} %get-tuple-element.32) | data formatting | bytes 1572864
  23.5 2.0 %reshape.4 = bf16[512,768]{1,0:T(8,128)(2,1)} reshape(bf16[512,12,64]{2,1,0:T(8,128)(2,1)S(1)} %bitcast.28) | data formatting | bytes 1572864
  25.6 0.0 copy-start
  25.6 0.0 reduce-scatter.4.cloned.1.call-update
  25.6 0.0 all-reduce.2.cloned.1.call-start
  25.7 26.0 %reduce-scatter.4.cloned.1.call-done = bf16[128,768]{1,0:T(8,128)(2,1)} async-done(((bf16[512,768]{1,0:T(8,128)(2,1)}), bf16[128,768]{1,0:T(8,128)(2,1)}) %reduce-scatter.4.cloned.1.call-update) | async-done | bytes 196624
  51.7 1.3 reshape.5
  52.9 1.0 copy.6
  54.0 0.0 all-reduce.2.cloned.1.call-update
  54.0 53.9 %all-reduce.2.cloned.1.call-done = bf16[12,64,128]{2,1,0:T(8,128)(2,1)} async-done(((bf16[12,64,128]{2,1,0:T(8,128)(2,1)}), bf16[12,64,128]{2,1,0:T(8,128)(2,1)}) %all-reduce.2.cloned.1.call-update) | async-done | bytes 196624 | tf_op jit(solution)/shard_map/psum | solution.py:27
  107.9 18.8 %all_gather.3 = bf16[12,64,512]{2,1,0:T(8,128)(2,1)S(1)} all-gather(bf16[12,64,128]{2,1,0:T(8,128)(2,1)} %all-reduce.2.cloned.1.call-done), channel_id=1, replica_groups=mesh['row'=8,'col'=4] {'col'}, dimensions={2}, use_global_device_ids=true | all-gather | bytes 983040 | tf_op jit(solution)/shard_map/all_gather | solution.py:31
  126.7 0.0 copy-done
  126.7 0.6 fusion.8
  127.3 14.4 %all_to_all.19 = bf16[4,128,512]{2,1,0:T(8,128)(2,1)S(1)} all-to-all(bf16[4,128,512]{2,1,0:T(8,128)(2,1)S(1)} %bitcast.31), channel_id=1, replica_groups=mesh['row'=8,'col'=4] {'col'}, dimensions={0} | all-to-all | bytes 1048576 | tf_op jit(solution)/shard_map/all_to_all | solution.py:36
  141.8 0.8 copy.7
  (13 shorter events, 0.1 us)
Async XLA Ops:
  6.5 45.1 %reduce-scatter.4.cloned.1.call-start = ((), (), s32[]{:S(2)}) async-start(), calls=%async_computation.3 | async-start | bytes 983040
  25.6 101.2 %copy-start = (bf16[12,64,512]{2,1,0:T(8,128)(2,1)S(1)}, bf16[12,64,512]{2,1,0:T(8,128)(2,1)}, u32[]{:S(2)}) copy-start(bf16[12,64,512]{2,1,0:T(8,128)(2,1)} %get-tuple-element.99) | copy-start | bytes 2359300
  25.6 82.3 %all-reduce.2.cloned.1.call-start = ((), (), s32[]{:S(2)}) async-start(), calls=%async_computation.2 | async-start | bytes 393216 | tf_op jit(solution)/shard_map/psum | solution.py:27
Sparse Core Ops, SparseCore 0:
  25.7 25.8 reduce-scatter.3
  54.7 53.1 all-reduce.1
where the time goes:
time: 150 us; the launch traced here: 149 us
  waiting for transfers between devices  80 us (53%)
  blocking collectives  33.2 us (22%)
  matrix products  14.5 us (10%)
  between operations  13.4 us (9%)
  local copies, waits for them, and re-layouts  7.3 us (5%)
    psum x1, waiting for transfers between devices, body(): readings = lax.psum(owned, 'row').astype(jnp.float32).astype(jnp.bfloat16)  53.9 us
    unnamed x3, waiting for transfers between devices  26 us
    all_gather x1, blocking collectives, body(): lax.all_gather(readings, 'col', axis=2, tiled=True)  18.8 us
    all_to_all x1, blocking collectives, body(): lax.all_to_all(rounded, 'col', split_axis=0, concat_axis=1, tiled=True)  14.4 us
    dot_general x12, matrix products, one_tier(): return jnp.dot(tier_fields, selector, preferred_element_type=jnp.float32)  13.9 us
    unnamed x6, local copies, waits for them, and re-layouts  6.33 us
  transfers between devices with their start and end apart: 2, of which 2 were waited for; matrix products, arithmetic and copies ran while one was open for 0% of the time, Pallas kernels for 0%

commit v1 on v0

--- a/solution.py
+++ b/solution.py
@@ -2,6 +2,12 @@
 import jax.numpy as jnp
 from jax import lax
 from jax.sharding import PartitionSpec as P
+
+
+def joined_along(tiles, dim):
+    tiles = jnp.moveaxis(tiles, 0, dim)
+    dims = tiles.shape
+    return tiles.reshape(*dims[:dim], dims[dim] * dims[dim + 1], *dims[dim + 2 :])
 
 
 def select_columns(fields, sensor_rows, first_pixel):
@@ -26,12 +32,26 @@
     )
     readings = lax.psum(owned, "row").astype(jnp.float32).astype(jnp.bfloat16)
     scale_factor = 1.0 / jnp.sqrt(jnp.float32(temps.shape[0] * temps.shape[1]))
-    summed = jnp.einsum(
-        "tsc,tsp->cp",
-        lax.all_gather(readings, "col", axis=2, tiled=True),
-        temps,
-        preferred_element_type=jnp.float32,
-    )
+    size, index, span = (lax.axis_size("col"), lax.axis_index("col"), readings.shape[2])
+    right = [(i, (i + 1) % size) for i in range(size)]
+    backward = [(i, (i - 1) % size) for i in range(size)]
+    half = size // 2
+    blocks = {}
+    from_left = from_right = readings
+    for step in range(half + 1):
+        next_left = lax.ppermute(from_left, "col", right) if step < half else None
+        next_right = lax.ppermute(from_right, "col", backward) if step < size - half - 1 else None
+        blocks[-step] = jnp.einsum(
+            "tsc,tsp->cp", from_left, temps, preferred_element_type=jnp.float32
+        )
+        if 0 < step < size - half:
+            blocks[step] = jnp.einsum(
+                "tsc,tsp->cp", from_right, temps, preferred_element_type=jnp.float32
+            )
+        from_left, from_right = (next_left, next_right)
+    blocks = jnp.stack([blocks[k] for k in sorted(blocks)])
+    blocks = blocks[(jnp.arange(size) - index + half) % size]
+    summed = joined_along(blocks, 0)
     rounded = (summed * scale_factor).astype(jnp.bfloat16)
     return lax.all_to_all(rounded, "col", split_axis=0, concat_axis=1, tiled=True)
 

time: 150 us -> 149 us (level)
  blocking collectives: 33.2 us -> 14.1 us
  waiting for transfers between devices: 80 us -> 91.5 us
  starting transfers between devices: 0.04 us -> 3.87 us
  matrix products: 14.5 us -> 16 us
    all_gather x1 -> x0, blocking collectives: 18.8 us -> none  [body(): lax.all_gather(readings, 'col', axis=2, tiled=True)]
    ppermute x0 -> x3, waiting for transfers between devices: none -> 11.6 us  [the longest x2 9.26 us: body(): next_left = lax.ppermute(from_left, 'col', right) if step < half else None]
    ppermute x0 -> x3, starting transfers between devices: none -> 3.83 us  [the longest x1 2.34 us: body(): lax.ppermute(from_right, 'col', backward)]
    dot_general x1 -> x4, matrix products: 0.6 us -> 2.12 us  [the longest x3 1.83 us: body(): jnp.einsum('tsc,tsp->cp', from_left, temps, preferred_element_type=jnp.fl...]
  transfers between devices with their start and end apart: 2 -> 5, of which waited for: 2 -> 5; matrix products, arithmetic and copies ran while one was open for 0% -> 1% of each run, Pallas kernels for 0% -> 0%
where the time goes in v1:
time: 149 us
  waiting for transfers between devices  91.5 us (61%)
  matrix products  16 us (11%)
  blocking collectives  14.1 us (9%)
  between operations  13.5 us (9%)
  local copies, waits for them, and re-layouts  8.36 us (6%)
  starting transfers between devices  3.87 us (3%)
    psum x1, waiting for transfers between devices, body(): readings = lax.psum(owned, 'row').astype(jnp.float32).astype(jnp.bfloat16)  53.9 us
    unnamed x3, waiting for transfers between devices  26 us
    all_to_all x1, blocking collectives, body(): lax.all_to_all(rounded, 'col', split_axis=0, concat_axis=1, tiled=True)  14.1 us
    dot_general x12, matrix products, one_tier(): return jnp.dot(tier_fields, selector, preferred_element_type=jnp.float32)  13.9 us
    ppermute x2, waiting for transfers between devices, body(): next_left = lax.ppermute(from_left, 'col', right) if step < half else None  9.26 us
    unnamed x6, local copies, waits for them, and re-layouts  6.34 us
  transfers between devices with their start and end apart: 5, of which 5 were waited for; matrix products, arithmetic and copies ran while one was open for 1% of the time, Pallas kernels for 0%

profile of v1, /device:TPU:0, one launch (start us, length us, event | category | flops | bytes accessed | tf_op | source)
XLA Modules:
  0.0 148.6 jit_solution(5023286662475918888)
XLA Ops:
  6.5 0.0 reduce-scatter.4.cloned.1.call-start
  6.5 0.8 broadcast_subtract_fusion
  7.3 14.2 %while.11 = (s32[]{:T(128)}, bf16[12,64,512]{2,1,0:T(8,128)(2,1)S(1)}, bf16[12,64,512]{2,1,0:T(8,128)(2,1)}, s32[12,512]{1,0:T(8,128)S(1)}, s32[]{:T(128)}) while((s32[]{:T(128)}, bf16[12,64,512]{2,1,0:T(8,128)(2,1)S(1)}, bf16[12,64,512]{2,1,0:T(8,128)(2,1)}, s32[12,512]{1,0:T(8,128)S(1)}, s32[]{:T(128)}) %tuple.21), condition=%wide.region_1.2_spmd.clone, body=%wide.region_0.1_spmd.clone.sunk | while | flops 33816576 | bytes 203841 | solution.py:23
  7.3 1.2 fusion.20
  8.5 1.2 fusion.20
  9.7 1.2 fusion.20
  10.9 1.2 fusion.20
  12.1 1.2 fusion.20
  13.2 1.2 fusion.20
  14.4 1.2 fusion.20
  15.6 1.2 fusion.20
  16.8 1.2 fusion.20
  18.0 1.2 fusion.20
  19.2 1.2 fusion.20
  20.4 1.2 fusion.20
  21.5 2.0 %copy.7 = bf16[12,64,512]{1,0,2:T(8,128)(2,1)S(1)} copy(bf16[12,64,512]{2,1,0:T(8,128)(2,1)S(1)} %get-tuple-element.32) | data formatting | bytes 1572864
  23.5 0.0 copy-start
  23.6 2.0 %reshape.68 = bf16[512,768]{1,0:T(8,128)(2,1)} reshape(bf16[512,12,64]{2,1,0:T(8,128)(2,1)S(1)} %bitcast.40) | data formatting | bytes 1572864
  25.6 0.0 reduce-scatter.4.cloned.1.call-update
  25.6 0.0 all-reduce.2.cloned.1.call-start
  25.7 26.0 %reduce-scatter.4.cloned.1.call-done = bf16[128,768]{1,0:T(8,128)(2,1)} async-done(((bf16[512,768]{1,0:T(8,128)(2,1)}), bf16[128,768]{1,0:T(8,128)(2,1)}) %reduce-scatter.4.cloned.1.call-update) | async-done | bytes 196624
  51.7 1.3 reshape.69
  52.9 1.0 copy.8
  54.0 0.0 all-reduce.2.cloned.1.call-update
  54.0 53.9 %all-reduce.2.cloned.1.call-done = bf16[12,64,128]{2,1,0:T(8,128)(2,1)} async-done(((bf16[12,64,128]{2,1,0:T(8,128)(2,1)}), bf16[12,64,128]{2,1,0:T(8,128)(2,1)}) %all-reduce.2.cloned.1.call-update) | async-done | bytes 196624 | tf_op jit(solution)/shard_map/psum | solution.py:33
  107.9 1.5 %collective-permute-start = (bf16[12,64,128]{2,1,0:T(8,128)(2,1)}, bf16[12,64,128]{2,1,0:T(8,128)(2,1)S(1)}, u32[]{:S(2)}, u32[]{:S(2)}) collective-permute-start(bf16[12,64,128]{2,1,0:T(8,128)(2,1)} %all-reduce.2.cloned.1.call-done), channel_id=1, source_target_pairs={{0,1},{1,2},{2,3},{3,0},{4,5},{5,6},{6,7},{7,4},{8,9},{9,10},{10,1... | collective-permute-start | bytes 589832 | tf_op jit(solution)/shard_map/ppermute | solution.py:42
  109.4 2.3 %collective-permute-start.2 = (bf16[12,64,128]{2,1,0:T(8,128)(2,1)}, bf16[12,64,128]{2,1,0:T(8,128)(2,1)S(1)}, u32[]{:S(2)}, u32[]{:S(2)}) collective-permute-start(bf16[12,64,128]{2,1,0:T(8,128)(2,1)} %all-reduce.2.cloned.1.call-done), channel_id=1, source_target_pairs={{0,3},{1,0},{2,1},{3,2},{4,7},{5,4},{6,5},{7,6},{8,11},{9,8},{10,9... | collective-permute-start | bytes 589832 | tf_op jit(solution)/shard_map/ppermute | solution.py:43
  111.8 0.0 copy-done
  111.8 1.2 convolution_bitcast_fusion.2
  113.0 4.7 %collective-permute-done = bf16[12,64,128]{2,1,0:T(8,128)(2,1)S(1)} collective-permute-done((bf16[12,64,128]{2,1,0:T(8,128)(2,1)}, bf16[12,64,128]{2,1,0:T(8,128)(2,1)S(1)}, u32[]{:S(2)}, u32[]{:S(2)}) %collective-permute-start) | collective-permute-done | bytes 196640 | tf_op jit(solution)/shard_map/ppermute | solution.py:42
  117.8 0.0 collective-permute-start.1
  117.8 0.3 convolution_bitcast_fusion.3
  118.1 2.3 %collective-permute-done.2 = bf16[12,64,128]{2,1,0:T(8,128)(2,1)S(1)} collective-permute-done((bf16[12,64,128]{2,1,0:T(8,128)(2,1)}, bf16[12,64,128]{2,1,0:T(8,128)(2,1)S(1)}, u32[]{:S(2)}, u32[]{:S(2)}) %collective-permute-start.2) | collective-permute-done | bytes 196640 | tf_op jit(solution)/shard_map/ppermute | solution.py:43
  120.4 0.3 convolution_bitcast_fusion.1
  120.7 4.5 %collective-permute-done.1 = bf16[12,64,128]{2,1,0:T(8,128)(2,1)S(1)} collective-permute-done((bf16[12,64,128]{2,1,0:T(8,128)(2,1)S(1)}, bf16[12,64,128]{2,1,0:T(8,128)(2,1)S(1)}, u32[]{:S(2)}, u32[]{:S(2)}) %collective-permute-start.1) | collective-permute-done | bytes 196640 | tf_op jit(solution)/shard_map/ppermute | solution.py:42
  125.2 0.3 convolution_bitcast_fusion.4
  125.5 0.1 pad_maximum_fusion
  125.6 0.6 gather_fusion
  126.2 0.1 multiply_convert_fusion
  126.4 14.1 %all_to_all.16 = bf16[4,128,512]{2,1,0:T(8,128)(2,1)S(1)} all-to-all(bf16[4,128,512]{2,1,0:T(8,128)(2,1)S(1)} %multiply_convert_fusion), channel_id=1, replica_groups=mesh['row'=8,'col'=4] {'col'}, dimensions={0} | all-to-all | bytes 1048576 | tf_op jit(solution)/shard_map/all_to_all | solution.py:56
  140.5 0.3 copy.5
  140.7 1.0 copy.6
  (15 shorter events, 0.1 us)
Async XLA Ops:
  6.5 45.1 %reduce-scatter.4.cloned.1.call-start = ((), (), s32[]{:S(2)}) async-start(), calls=%async_computation.3 | async-start | bytes 983040
  23.5 88.2 %copy-start = (bf16[12,64,512]{2,1,0:T(8,128)(2,1)S(1)}, bf16[12,64,512]{2,1,0:T(8,128)(2,1)}, u32[]{:S(2)}) copy-start(bf16[12,64,512]{2,1,0:T(8,128)(2,1)} %get-tuple-element.93) | copy-start | bytes 2359300
  25.6 82.3 %all-reduce.2.cloned.1.call-start = ((), (), s32[]{:S(2)}) async-start(), calls=%async_computation.2 | async-start | bytes 393216 | tf_op jit(solution)/shard_map/psum | solution.py:33
  107.9 9.8 %collective-permute-start = (bf16[12,64,128]{2,1,0:T(8,128)(2,1)}, bf16[12,64,128]{2,1,0:T(8,128)(2,1)S(1)}, u32[]{:S(2)}, u32[]{:S(2)}) collective-permute-start(bf16[12,64,128]{2,1,0:T(8,128)(2,1)} %all-reduce.2.cloned.1.call-done), channel_id=1, source_target_pairs={{0,1},{1,2},{2,3},{3,0},{4,5},{5,6},{6,7},{7,4},{8,9},{9,10},{10,1... | collective-permute-start | bytes 589832 | tf_op jit(solution)/shard_map/ppermute | solution.py:42
  109.4 11.0 %collective-permute-start.2 = (bf16[12,64,128]{2,1,0:T(8,128)(2,1)}, bf16[12,64,128]{2,1,0:T(8,128)(2,1)S(1)}, u32[]{:S(2)}, u32[]{:S(2)}) collective-permute-start(bf16[12,64,128]{2,1,0:T(8,128)(2,1)} %all-reduce.2.cloned.1.call-done), channel_id=1, source_target_pairs={{0,3},{1,0},{2,1},{3,2},{4,7},{5,4},{6,5},{7,6},{8,11},{9,8},{10,9... | collective-permute-start | bytes 589832 | tf_op jit(solution)/shard_map/ppermute | solution.py:43
  117.8 7.5 %collective-permute-start.1 = (bf16[12,64,128]{2,1,0:T(8,128)(2,1)S(1)}, bf16[12,64,128]{2,1,0:T(8,128)(2,1)S(1)}, u32[]{:S(2)}, u32[]{:S(2)}) collective-permute-start(bf16[12,64,128]{2,1,0:T(8,128)(2,1)S(1)} %collective-permute-done), channel_id=1, source_target_pairs={{0,1},{1,2},{2,3},{3,0},{4,5},{5,6},{6,7},{7,4},{8,9},{9,10},{10,1... | collective-permute-start | bytes 589832 | tf_op jit(solution)/shard_map/ppermute | solution.py:42
Sparse Core Ops, SparseCore 0:
  25.7 25.8 reduce-scatter.3
  54.7 53.1 all-reduce.1
